TPU v7x, 256 devices: a whole 4x4x8 slice. The times are simulated.
256 devices in a mesh: space: 4 (over y_hi, core), shard: 64 (over x, z, y_lo).
Axes of the slice: x: 4, y: 4 (y_hi: 2, y_lo: 2; y = y_hi * 2 + y_lo), z: 8, core: 2. Of those that a mesh axis runs over, the one named last changes fastest.
Arguments:
- volume_field: float32 [2, 16, 16, 1024, 128], P(None, None, 'space', 'shard'), may hold values from -6 to 6
- source: float32 [2, 16, 16, 1024, 128], P(None, None, 'space', 'shard'), may hold values from -6 to 6
- material: int32 [16, 1024, 128], P('space', 'shard'), may hold values from 0 to 7
- mat_real: float32 [8], replicated, may hold values from 0.5 to 4
- mat_loss: float32 [8], replicated, may hold values from 0.1 to 1.5
- surface_map: int32 [4096, 128], P(('space', 'shard')), may hold values from 0 to 8191
- near_boxes: int32 [4096, 4], P(('space', 'shard')), may hold values from 0 to 4095, as said below
- near_blocks: bfloat16 [4, 256, 256], replicated, may hold values from -0.1875 to 0.1875
- radiate: bfloat16 [2, 128, 512], replicated, may hold values from -0.375 to 0.375
- interp: bfloat16 [512, 2048], replicated, may hold values from -0.25 to 0.25
- phase_angle: float32 [8, 2048], replicated, may hold values from -3.140625 to 3.140625
- far_parents: int32 [512, 8], replicated, may hold values from 0 to 511
- far_kind: int32 [512, 8], replicated, may hold values from 0 to 315
- translate: float32 [316, 2, 2048], P(None, None, 'shard'), may hold values from -0.18 to 0.18
Outputs:
- volume_out: float32 [2, 16, 16, 1024, 128], P(None, None, 'space', 'shard')
- forcing: float32 [4096, 16, 256], P(('space', 'shard'))
Inputs may be any that keep to these rules, and one draw needn't show every extreme that they name: near_boxes[b, 0] = b; every other entry is a box of the same group of 1024 boxes (boxes g * 1024 to (g + 1) * 1024 - 1) whose index lies from 16 below to 31 above the first box of b's run of 16 boxes.
All inputs are finite; a program needn't handle non-finite values.
Results may differ from a plain program's by a relative error of at most 0.015.
Values may be sent and summed in bfloat16 or wider, within the bound.
A program may use at most 128 MiB of HBM per device.

v0:
```python
import math
import jax
import jax.numpy as jnp
from jax import lax
from jax.sharding import PartitionSpec as P

relaxation = 0.8


def extended(array, sides, width):
    edges = {}
    for axis, dim in sides:
        peers, length = (lax.axis_size(axis), array.shape[dim])
        up = [(i, (i + 1) % peers) for i in range(peers - 1)]
        last = lax.slice_in_dim(array, length - width, length, axis=dim)
        leading = lax.slice_in_dim(array, 0, width, axis=dim)
        edges[dim] = (
            lax.ppermute(last, axis, up),
            lax.ppermute(leading, axis, [(b, a) for a, b in up]),
        )
    done = []
    for _, dim in sides:
        low, high = edges[dim]
        around = [(width, width) if d in done else (0, 0) for d in range(array.ndim)]
        array = jnp.concatenate([jnp.pad(low, around), array, jnp.pad(high, around)], axis=dim)
        done.append(dim)
    return array


def padded_2(array, sides, width):
    for axis, dim in sides:
        peers, length = (lax.axis_size(axis), array.shape[dim])
        up = [(i, (i + 1) % peers) for i in range(peers - 1)]
        down = [(j, i) for i, j in up]
        last = lax.slice_in_dim(array, length - width, length, axis=dim)
        leading = lax.slice_in_dim(array, 0, width, axis=dim)
        before = lax.ppermute(last, axis, up)
        after = lax.ppermute(leading, axis, down)
        array = jnp.concatenate([before, array, after], axis=dim)
    return array


def sent_to_all(array, axis):
    copies = jnp.broadcast_to(array, (lax.axis_size(axis), *array.shape))
    return lax.all_to_all(copies, axis, split_axis=0, concat_axis=0, tiled=True)


def joined_along(tiles, dim):
    tiles = jnp.moveaxis(tiles, 0, dim)
    lengths = tiles.shape
    return tiles.reshape(*lengths[:dim], lengths[dim] * lengths[dim + 1], *lengths[dim + 2 :])


def gathered_copies(array, axis, dim):
    tiles = sent_to_all(array, axis)
    return joined_along(tiles, dim)


def neighbour_sum(padded):
    core = padded[:, :, 1:-1, 1:-1]
    result = padded[:, :, 2:, 1:-1] + padded[:, :, :-2, 1:-1]
    result = result + padded[:, :, 1:-1, 2:] + padded[:, :, 1:-1, :-2]
    zero_layer = jnp.zeros(core.shape[:-1] + (1,), core.dtype)
    upper = jnp.concatenate([core[..., 1:], zero_layer], axis=-1)
    lower = jnp.concatenate([zero_layer, core[..., :-1]], axis=-1)
    return result + upper + lower


def relax_sweep(current, neighbours, source, diagonal_coef, loss_coef):
    real_part = diagonal_coef * current[0] - neighbours[0] - loss_coef * current[1]
    imag_part = diagonal_coef * current[1] - neighbours[1] + loss_coef * current[0]
    applied = jnp.stack([real_part, imag_part])
    return current + relaxation * (source - applied) / diagonal_coef


def block_matrix(radiate):
    upper = jnp.concatenate([radiate[0], radiate[1]], axis=1)
    lower = jnp.concatenate([-radiate[1], radiate[0]], axis=1)
    return jnp.concatenate([upper, lower], axis=0)


def aggregate(leaf_rows, interp, cosine, sine_part):
    parent_count = leaf_rows.shape[0] // 8
    excite = leaf_rows.shape[1]
    spread = jnp.dot(
        leaf_rows.reshape(-1, interp.shape[0]), interp, preferred_element_type=jnp.float32
    )
    spread = spread.reshape(parent_count, 8, excite, 2, interp.shape[1])
    cosine_wide = cosine[None, :, None, :]
    sine_wide = sine_part[None, :, None, :]
    real_part = jnp.sum(cosine_wide * spread[:, :, :, 0] - sine_wide * spread[:, :, :, 1], axis=1)
    imag_part = jnp.sum(sine_wide * spread[:, :, :, 0] + cosine_wide * spread[:, :, :, 1], axis=1)
    return jnp.stack([real_part, imag_part], axis=2).astype(jnp.bfloat16)


def combine_far(sources, table):
    real_table = table[:, :, None, 0]
    imag_table = table[:, :, None, 1]
    real_part = jnp.sum(real_table * sources[:, :, :, 0] - imag_table * sources[:, :, :, 1], axis=1)
    imag_part = jnp.sum(imag_table * sources[:, :, :, 0] + real_table * sources[:, :, :, 1], axis=1)
    return jnp.stack([real_part, imag_part], axis=2)


def disaggregate(incoming_rows, interp, cosine, sine_part, weights):
    parent_count = incoming_rows.shape[0]
    excite = incoming_rows.shape[1]
    widened = incoming_rows.astype(jnp.float32)[:, None]
    cosine_wide = cosine[None, :, None, :]
    sine_wide = sine_part[None, :, None, :]
    real_part = cosine_wide * widened[:, :, :, 0] + sine_wide * widened[:, :, :, 1]
    imag_part = cosine_wide * widened[:, :, :, 1] - sine_wide * widened[:, :, :, 0]
    shifted = jnp.stack([real_part, imag_part], axis=3).astype(jnp.bfloat16)
    leaf_in = jnp.dot(
        shifted.reshape(-1, interp.shape[1]), interp.T, preferred_element_type=jnp.float32
    ).astype(jnp.bfloat16)
    leaf_in = leaf_in.reshape(parent_count * 8 * excite, 2 * interp.shape[0])
    far_part = jnp.dot(leaf_in, weights.T, preferred_element_type=jnp.float32)
    return far_part.reshape(parent_count * 8, excite, weights.shape[0])


def select_cells(flat_field, cell_keys):
    cell_total = flat_field.shape[1]
    block_cells = math.gcd(cell_total, 1024)
    block_total = cell_total // block_cells
    positions = jnp.arange(block_cells, dtype=jnp.int32)

    def add_block(block_index, total):
        first = block_index * block_cells
        piece = lax.dynamic_slice_in_dim(flat_field, first, block_cells, 1)
        selector = (cell_keys[None, :] == (first + positions)[:, None]).astype(jnp.bfloat16)
        return total + jnp.dot(piece, selector, preferred_element_type=jnp.float32)

    empty = jnp.zeros((flat_field.shape[0], cell_keys.shape[0]), jnp.float32)
    return lax.fori_loop(0, block_total, add_block, empty)


def shards(
    volume_field,
    source,
    material,
    mat_real,
    mat_loss,
    surface_map,
    near_boxes,
    near_blocks,
    radiate,
    interp,
    phase_angle,
    far_parents,
    far_kind,
    translate,
):
    excite = volume_field.shape[1]
    cells_x = volume_field.shape[2]
    cells_y = volume_field.shape[3]
    cells_z = volume_field.shape[4]
    diagonal_coef = jnp.full(material.shape, 6.0, jnp.float32)
    loss_coef = jnp.zeros(material.shape, jnp.float32)
    for material_kind in range(mat_real.shape[0]):
        present = material == material_kind
        diagonal_coef = diagonal_coef + jnp.where(present, mat_real[material_kind], 0.0)
        loss_coef = loss_coef + jnp.where(present, mat_loss[material_kind], 0.0)
    current = volume_field
    for sweep_index in range(2):
        padded = extended(current.astype(jnp.bfloat16), (("space", 2), ("shard", 3)), 1).astype(
            current.dtype
        )
        current = relax_sweep(current, neighbour_sum(padded), source, diagonal_coef, loss_coef)
    box_count = surface_map.shape[0]
    unknowns = surface_map.shape[1]
    flat_field = current.reshape(2 * excite, cells_x * cells_y * cells_z).astype(jnp.bfloat16)
    sampled = select_cells(flat_field, surface_map.reshape(-1)).astype(jnp.bfloat16)
    sampled = sampled.reshape(2, excite, box_count, unknowns)
    currents = jnp.transpose(sampled, (2, 1, 0, 3)).reshape(box_count, excite, 2 * unknowns)
    device_rank = lax.axis_index("space") * lax.axis_size("shard") + lax.axis_index("shard")
    beside_all = padded_2(currents, (("shard", 0),), box_count)
    local_near = near_boxes - (device_rank * box_count - box_count)
    near_force = jnp.zeros((box_count, excite, 2 * unknowns), jnp.float32)
    for slot_index in range(near_boxes.shape[1]):
        picked = jnp.take(beside_all, local_near[:, slot_index], axis=0).reshape(
            box_count * excite, 2 * unknowns
        )
        near_force = near_force + jnp.dot(
            picked, near_blocks[slot_index], preferred_element_type=jnp.float32
        ).reshape(box_count, excite, 2 * unknowns)
    weights = block_matrix(radiate)
    leaf_dirs = interp.shape[0]
    leaf = jnp.dot(
        currents.reshape(box_count * excite, 2 * unknowns),
        weights,
        preferred_element_type=jnp.float32,
    ).astype(jnp.bfloat16)
    leaf = leaf.reshape(box_count, excite, 2, leaf_dirs)
    cosine = jnp.cos(phase_angle)
    sine_part = jnp.sin(phase_angle)
    parent_patterns = aggregate(leaf, interp, cosine, sine_part)
    directed = lax.all_to_all(parent_patterns, "shard", split_axis=3, concat_axis=0, tiled=True)
    group_parents = directed.shape[0]
    group_index = lax.axis_index("space")
    target_ids = lax.dynamic_slice_in_dim(
        far_parents, group_index * group_parents, group_parents, 0
    )
    target_kinds = lax.dynamic_slice_in_dim(far_kind, group_index * group_parents, group_parents, 0)
    table = jnp.take(translate, target_kinds, axis=0)
    gathered = gathered_copies(directed, "space", 0)
    sources = jnp.take(gathered, target_ids, axis=0).astype(jnp.float32)
    incoming = combine_far(sources, table).astype(jnp.bfloat16)
    far_force = disaggregate(
        lax.all_to_all(incoming, "shard", split_axis=0, concat_axis=3, tiled=True),
        interp,
        cosine,
        sine_part,
        weights,
    )
    forcing = near_force + far_force
    return (current, forcing)


def solution(mesh):
    return jax.shard_map(
        shards,
        mesh=mesh,
        in_specs=(
            P(None, None, "space", "shard", None),
            P(None, None, "space", "shard", None),
            P("space", "shard", None),
            P(),
            P(),
            P(("space", "shard"), None),
            P(("space", "shard"), None),
            P(),
            P(),
            P(),
            P(),
            P(),
            P(),
            P(None, None, "shard"),
        ),
        out_specs=(P(None, None, "space", "shard", None), P(("space", "shard"), None, None)),
        check_vma=False,
    )
```

profile of v0, /device:TPU:1, one launch (start us, length us, event | category | flops | bytes accessed | tf_op | source)
XLA Modules:
  0.0 238.4 jit_solution(12585446366366786209)
XLA Ops:
  4.2 4.6 %collective-permute-start = (bf16[2,16,4,1,128]{4,3,2,1,0:T(2,128)(2,1)S(1)}, bf16[2,16,4,1,128]{4,3,2,1,0:T(2,128)(2,1)S(1)}, u32[]{:S(2)}, u32[]{:S(2)}) collective-permute-start(bf16[2,16,4,1,128]{4,3,2,1,0:T(2,128)(2,1)S(1)} %get-tuple-element.172), channel_id=1, source_target_pairs={{0,1},{1,2},{2,3},{3,4},{4,5},{5,6},{6,7},{7,8},{8,9},{9,10},{10,1... | collective-permute-start | bytes 98312 | tf_op jit(solution)/shard_map/ppermute | solution.py:18
  8.9 5.0 %collective-permute-start.2 = (bf16[2,16,1,16,128]{4,3,2,1,0:T(8,128)(2,1)S(1)}, bf16[2,16,1,16,128]{4,3,2,1,0:T(8,128)(2,1)S(1)}, u32[]{:S(2)}, u32[]{:S(2)}) collective-permute-start(bf16[2,16,1,16,128]{4,3,2,1,0:T(8,128)(2,1)S(1)} %get-tuple-element.171), channel_id=1, source_target_pairs={{64,0},{128,64},{192,128},{65,1},{129,65},{193,129},{66,2},{130,66... | collective-permute-start | bytes 393224 | tf_op jit(solution)/shard_map/ppermute | solution.py:19
  13.9 3.0 %collective-permute-start.1 = (bf16[2,16,1,16,128]{4,3,2,1,0:T(8,128)(2,1)S(1)}, bf16[2,16,1,16,128]{4,3,2,1,0:T(8,128)(2,1)S(1)}, u32[]{:S(2)}, u32[]{:S(2)}) collective-permute-start(bf16[2,16,1,16,128]{4,3,2,1,0:T(8,128)(2,1)S(1)} %get-tuple-element.170), channel_id=1, source_target_pairs={{0,64},{64,128},{128,192},{1,65},{65,129},{129,193},{2,66},{66,130... | collective-permute-start | bytes 393224 | tf_op jit(solution)/shard_map/ppermute | solution.py:18
  21.7 5.2 %select_add_fusion.1 = (f32[4,16,128]{2,1,0:T(8,128)S(1)}, pred[4,16,128]{2,1,0:T(8,128)(4,1)S(1)}, pred[4,16,128]{2,1,0:T(8,128)(4,1)S(1)}, pred[4,16,128]{2,1,...) fusion(f32[]{:T(128)} %bitcast.7, f32[]{:T(128)} %bitcast.6, ...), kind=kLoop, calls=%fused_computation.118 | loop fusion | flops 196608 | bytes 131104 | tf_op jit(solution)/shard_map/add | solution.py:161
  26.9 5.0 %select_add_fusion = f32[4,16,128]{2,1,0:T(8,128)S(1)} fusion(pred[4,16,128]{2,1,0:T(8,128)(4,1)S(1)} %get-tuple-element.151, pred[4,16,128]{2,1,0:T(8,128)(4,1)S(1)} %get-tuple-element.150, pred[4,16,128]{2,1,0:T(8,128)(4,1)S(1)} %get-tuple-element.149, pred[4,16,128]{2,1,0:T(8,128)(4,1)S(1)} %get-tuple-element.148, ...), kind=kLoop, calls=%fused_computation.117 | loop fusion | flops 122880 | bytes 98336 | tf_op jit(solution)/shard_map/add | solution.py:162
  38.1 4.6 %collective-permute-start.4 = (bf16[2,16,4,1,128]{4,3,2,1,0:T(2,128)(2,1)}, bf16[2,16,4,1,128]{4,3,2,1,0:T(2,128)(2,1)}, u32[]{:S(2)}, u32[]{:S(2)}) collective-permute-start(bf16[2,16,4,1,128]{4,3,2,1,0:T(2,128)(2,1)} %get-tuple-element.168), channel_id=1, source_target_pairs={{0,1},{1,2},{2,3},{3,4},{4,5},{5,6},{6,7},{7,8},{8,9},{9,10},{10,1... | collective-permute-start | bytes 98312 | tf_op jit(solution)/shard_map/ppermute | solution.py:18
  44.6 5.3 %collective-permute-start.5 = (bf16[2,16,1,16,128]{4,3,2,1,0:T(8,128)(2,1)}, bf16[2,16,1,16,128]{4,3,2,1,0:T(8,128)(2,1)}, u32[]{:S(2)}, u32[]{:S(2)}) collective-permute-start(bf16[2,16,1,16,128]{4,3,2,1,0:T(8,128)(2,1)} %get-tuple-element.166), channel_id=1, source_target_pairs={{0,64},{64,128},{128,192},{1,65},{65,129},{129,193},{2,66},{66,130... | collective-permute-start | bytes 393224 | tf_op jit(solution)/shard_map/ppermute | solution.py:18
  51.8 7.5 %gather_fusion = f32[1024,2,32]{2,1,0:T(2,128)} fusion(f32[316,2,32]{2,1,0:T(2,128)S(1)} %copy.108, s32[1024]{0:T(1024)S(1)} %broadcast_clamp_fusion.1), kind=kCustom, calls=%fused_computation.4 | custom fusion | bytes 528384 | tf_op jit(solution)/shard_map/jit(_take)/gather | solution.py:204
  66.0 12.9 %while.14 = (s32[]{:T(128)}, f32[32,2048]{1,0:T(8,128)S(1)}, bf16[32,8192]{1,0:T(8,128)(2,1)S(1)}, s32[16,128]{1,0:T(8,128)S(1)}, s32[]{:T(128)}, /*index=5*/s32[]{:T(128)}, s32[]{:T(128)}, s32[]{:T(128)}) while((s32[]{:T(128)}, f32[32,2048]{1,0:T(8,128)S(1)}, bf16[32,8192]{1,0:T(8,128)(2,1)S(1)}, s32[16,128]{1,0:T(8,128)S(1)}, ...), condition=%wide.region_1.2_spmd.clone, body=%wide.region_0.1_spmd.clone.sunk | while | flops 136446976 | bytes 606365 | solution.py:134
  83.0 3.7 %copy.113 = bf16[2,16,2,2048]{1,2,0,3:T(2,128)(2,1)} copy(bf16[2,16,2,2048]{3,1,0,2:T(8,128)(2,1)S(1)} %pad_maximum_fusion.2) | data formatting | bytes 524288 | tf_op jit(solution)/shard_map/stack | solution.py:93
  86.6 7.3 %reshape.176 = bf16[64,2,1024]{2,1,0:T(2,128)(2,1)} reshape(bf16[2048,2,2,16]{3,2,1,0:T(2,128)(2,1)} %bitcast.144) | data formatting | bytes 524288
  94.0 16.2 %all-to-all-start = ((bf16[64,2,1024]{2,1,0:T(2,128)(2,1)}), bf16[64,2,1024]{2,1,0:T(2,128)(2,1)S(1)}, u32[]{:S(2)}, u32[]{:S(2)}) async-start(bf16[64,2,1024]{2,1,0:T(2,128)(2,1)} %reshape.176), calls=%async_computation | async-start | bytes 524288 | tf_op jit(solution)/shard_map/all_to_all | solution.py:197
  111.4 9.3 %all-to-all-done = bf16[64,2,1024]{2,1,0:T(2,128)(2,1)S(1)} async-done(((bf16[64,2,1024]{2,1,0:T(2,128)(2,1)}), bf16[64,2,1024]{2,1,0:T(2,128)(2,1)S(1)}, u32[]{:S(2)}, u32[]{:S(2)}) %all-to-all-start) | async-done | bytes 262176 | tf_op jit(solution)/shard_map/all_to_all | solution.py:197
  120.7 2.4 %reshape.177 = bf16[2048,2,2,16]{3,2,1,0:T(2,128)(2,1)} reshape(bf16[64,2,1024]{2,1,0:T(2,128)(2,1)S(1)} %all-to-all-done) | data formatting | bytes 524288
  123.1 5.0 %copy.126 = bf16[2,16,2,64,32]{4,1,2,0,3:T(8,128)(2,1)S(1)} copy(bf16[2,16,2,64,32]{1,2,0,4,3:T(2,128)(2,1)} %bitcast.145) | data formatting | bytes 524288 | tf_op jit(solution)/shard_map/all_to_all | solution.py:197
  130.5 3.5 %all-to-all-start.1 = ((bf16[4,128,16,2,32]{1,4,3,2,0:T(8,128)(2,1)}), bf16[4,128,16,2,32]{1,4,3,2,0:T(8,128)(2,1)S(1)}, u32[]{:S(2)}, u32[]{:S(2)}) async-start(bf16[4,128,16,2,32]{1,4,3,2,0:T(8,128)(2,1)} %broadcast_in_dim.151), calls=%async_computation.1 | async-start | bytes 2097152 | tf_op jit(solution)/shard_map/all_to_all | solution.py:45
  135.0 2.9 %collective-permute-start.8 = (bf16[16,16,256]{2,1,0:T(8,128)(2,1)S(1)}, bf16[16,16,256]{2,1,0:T(8,128)(2,1)S(1)}, u32[]{:S(2)}, u32[]{:S(2)}) collective-permute-start(bf16[16,16,256]{2,1,0:T(8,128)(2,1)S(1)} %reshape.102), channel_id=1, source_target_pairs={{0,1},{1,2},{2,3},{3,4},{4,5},{5,6},{6,7},{7,8},{8,9},{9,10},{10,1... | collective-permute-start | bytes 393224 | tf_op jit(solution)/shard_map/ppermute | solution.py:37
  139.3 12.0 %collective-permute-done.8 = bf16[16,16,256]{2,1,0:T(8,128)(2,1)S(1)} collective-permute-done((bf16[16,16,256]{2,1,0:T(8,128)(2,1)S(1)}, bf16[16,16,256]{2,1,0:T(8,128)(2,1)S(1)}, u32[]{:S(2)}, u32[]{:S(2)}) %collective-permute-start.8) | collective-permute-done | bytes 131104 | tf_op jit(solution)/shard_map/ppermute | solution.py:37
  153.3 2.2 gather_fusion.5
  155.5 6.4 %copy.117 = bf16[4,128,16,2,32]{4,2,3,1,0:T(8,128)(2,1)} copy(bf16[4,128,16,2,32]{1,4,3,2,0:T(8,128)(2,1)S(1)} %all-to-all-done.1) | data formatting | bytes 2097152 | tf_op jit(solution)/shard_map/all_to_all | solution.py:45
  161.9 12.0 %gather_fusion.1 = bf16[1024,16,2,32]{3,1,2,0:T(8,128)(2,1)} fusion(bf16[512,16,2,32]{3,1,2,0:T(8,128)(2,1)} %bitcast.142, s32[1024]{0:T(1024)S(1)} %broadcast_clamp_fusion), kind=kCustom, calls=%fused_computation.5 | custom fusion | bytes 4198400 | tf_op jit(solution)/shard_map/jit(_take)/gather | solution.py:206
  173.9 5.9 %fusion.11 = f32[128,8,16,2,32]{4,2,1,0,3:T(8,128)S(1)} fusion(bf16[128,8,16,2,32]{4,2,3,1,0:T(8,128)(2,1)} %bitcast.143, pred[128,8]{1,0:T(8,128)(4,1)S(1)} %copy.110), kind=kLoop, calls=%fused_computation.18 | loop fusion | flops 2097152 | bytes 6292480 | tf_op jit(solution)/shard_map/convert_element_type | solution.py:206
  179.9 3.8 %subtract_reduce_fusion = (bf16[128,16,32]{2,1,0:T(8,128)(2,1)S(1)}, bf16[128,16,32]{2,1,0:T(8,128)(2,1)S(1)}) fusion(f32[128,8,16,2,32]{4,2,1,0,3:T(8,128)S(1)} %fusion.11, f32[128,8,32]{2,1,0:T(8,128)S(1)} %copy-done.7, f32[128,8,32]{2,1,0:T(8,128)S(1)} %copy-done.6), kind=kLoop, calls=%fused_computation.20 | loop fusion | flops 4063232 | bytes 4718592 | tf_op jit(solution)/shard_map/reduce_sum | solution.py:99
  187.2 7.5 %all-to-all-start.2 = ((bf16[64,2,1024]{2,1,0:T(2,128)(2,1)}), bf16[64,2,1024]{2,1,0:T(2,128)(2,1)S(1)}, u32[]{:S(2)}, u32[]{:S(2)}) async-start(bf16[64,2,1024]{2,1,0:T(2,128)(2,1)} %reshape.178), calls=%async_computation.2 | async-start | bytes 524288 | tf_op jit(solution)/shard_map/all_to_all | solution.py:209
  199.7 2.2 gather_fusion.2
  207.0 2.5 %copy.122 = f32[128,16,2,32]{3,1,2,0:T(8,128)} copy(bf16[128,16,2,32]{0,3,2,1:T(8,128)(2,1)S(1)} %copy.121) | data formatting | bytes 786432 | tf_op jit(solution)/shard_map/convert_element_type | solution.py:107
  209.5 4.2 %copy.123 = f32[2,16,2,64,32]{4,3,1,2,0:T(8,128)} copy(f32[2,16,2,64,32]{4,1,2,0,3:T(8,128)} %bitcast.146) | data formatting | bytes 1048576 | tf_op jit(solution)/shard_map/convert_element_type | solution.py:107
  213.7 2.5 %reshape.104 = f32[2,1,16,2,2048]{4,2,3,0,1:T(8,128)S(1)} reshape(f32[2,16,2,64,32]{4,3,1,2,0:T(8,128)} %copy.123) | data formatting | bytes 1048576 | tf_op jit(solution)/shard_map/convert_element_type | solution.py:107
  216.3 4.4 %add_convert_fusion = (bf16[2,8,16,1,2048]{4,3,2,1,0:T(2,128)(2,1)S(1)}, bf16[2,8,16,1,2048]{4,3,2,1,0:T(2,128)(2,1)S(1)}) fusion(f32[2,16,2048]{2,1,0:T(8,128)S(1)} %get-tuple-element.165, f32[8,2048]{1,0:T(8,128)S(1)} %copy-done.13, f32[2,16,2048]{2,1,0:T(8,128)S(1)} %get-tuple-element.164, f32[8,2048]{1,0:T(8,128)S(1)} %copy-done.11), kind=kLoop, calls=%fused_computation.33 | loop fusion | flops 4194304 | bytes 2752512 | tf_op jit(solution)/shard_map/convert.3
  220.7 5.2 %pad_maximum_fusion = bf16[2,8,16,2,2048]{4,3,2,1,0:T(2,128)(2,1)} fusion(bf16[2,8,16,1,2048]{4,3,2,1,0:T(2,128)(2,1)S(1)} %get-tuple-element.163, bf16[2,8,16,1,2048]{4,3,2,1,0:T(2,128)(2,1)S(1)} %get-tuple-element.162), kind=kLoop, calls=%fused_computation.29 | loop fusion | flops 4194304 | bytes 4194304 | tf_op jit(solution)/shard_map/stack | solution.py:112
  225.9 4.1 %convert_element_type.77 = bf16[512,2048]{1,0:T(8,128)(2,1)} reshape(bf16[2,8,16,2,2048]{4,3,2,1,0:T(2,128)(2,1)} %pad_maximum_fusion) | data formatting | bytes 4194304 | tf_op jit(solution)/shard_map/convert_element_type | solution.py:112
  230.0 3.7 %convolution_convert_fusion = bf16[512,512]{1,0:T(8,128)(2,1)} fusion(bf16[512,2048]{1,0:T(8,128)(2,1)} %convert_element_type.77, bf16[512,2048]{1,0:T(8,128)(2,1)S(1)} %copy-done), kind=kOutput, calls=%fused_computation.36 | convolution fusion | flops 1074003968 | bytes 4718592 | tf_op jit(solution)/shard_map/dot_general | solution.py:113
  (147 shorter events, 67.5 us)
Async XLA Ops:
  0.6 80.3 %copy-start = (bf16[512,2048]{1,0:T(8,128)(2,1)S(1)}, bf16[512,2048]{1,0:T(8,128)(2,1)}, u32[]{:S(2)}) copy-start(bf16[512,2048]{1,0:T(8,128)(2,1)} %param.27) | copy-start | bytes 6291460
  0.6 16.3 %copy-start.14 = (bf16[2,128,512]{2,1,0:T(8,128)(2,1)S(1)}, bf16[2,128,512]{2,1,0:T(8,128)(2,1)}, u32[]{:S(2)}) copy-start(bf16[2,128,512]{2,1,0:T(8,128)(2,1)} %param.26) | copy-start | bytes 786436
  0.7 17.7 %copy-start.20 = (f32[8]{0:T(128)S(1)}, f32[8]{0:T(128)}, u32[]{:S(2)}) copy-start(f32[8]{0:T(128)} %param.21) | copy-start | bytes 100
  0.7 18.3 %copy-start.21 = (f32[8]{0:T(128)S(1)}, f32[8]{0:T(128)}, u32[]{:S(2)}) copy-start(f32[8]{0:T(128)} %param.22) | copy-start | bytes 100
  0.7 19.0 %copy-start.19 = (f32[8,2048]{1,0:T(8,128)S(1)}, f32[8,2048]{1,0:T(8,128)}, u32[]{:S(2)}) copy-start(f32[8,2048]{1,0:T(8,128)} %param.28) | copy-start | bytes 196612
  0.7 21.0 %copy-start.22 = (s32[4,16,128]{2,1,0:T(8,128)S(1)}, s32[4,16,128]{2,1,0:T(8,128)}, u32[]{:S(2)}) copy-start(s32[4,16,128]{2,1,0:T(8,128)} %param.20) | copy-start | bytes 98308
  2.9 29.0 %collective-permute-start.3 = (bf16[2,16,4,1,128]{4,3,2,1,0:T(2,128)(2,1)}, bf16[2,16,4,1,128]{4,3,2,1,0:T(2,128)(2,1)S(1)}, u32[]{:S(2)}, u32[]{:S(2)}) collective-permute-start(bf16[2,16,4,1,128]{4,3,2,1,0:T(2,128)(2,1)} %get-tuple-element.173), channel_id=1, source_target_pairs={{1,0},{2,1},{3,2},{4,3},{5,4},{6,5},{7,6},{8,7},{9,8},{10,9},{11,1... | collective-permute-start | bytes 98312 | tf_op jit(solution)/shard_map/ppermute | solution.py:19
  4.2 27.7 %collective-permute-start = (bf16[2,16,4,1,128]{4,3,2,1,0:T(2,128)(2,1)S(1)}, bf16[2,16,4,1,128]{4,3,2,1,0:T(2,128)(2,1)S(1)}, u32[]{:S(2)}, u32[]{:S(2)}) collective-permute-start(bf16[2,16,4,1,128]{4,3,2,1,0:T(2,128)(2,1)S(1)} %get-tuple-element.172), channel_id=1, source_target_pairs={{0,1},{1,2},{2,3},{3,4},{4,5},{5,6},{6,7},{7,8},{8,9},{9,10},{10,1... | collective-permute-start | bytes 98312 | tf_op jit(solution)/shard_map/ppermute | solution.py:18
  8.9 23.1 %collective-permute-start.2 = (bf16[2,16,1,16,128]{4,3,2,1,0:T(8,128)(2,1)S(1)}, bf16[2,16,1,16,128]{4,3,2,1,0:T(8,128)(2,1)S(1)}, u32[]{:S(2)}, u32[]{:S(2)}) collective-permute-start(bf16[2,16,1,16,128]{4,3,2,1,0:T(8,128)(2,1)S(1)} %get-tuple-element.171), channel_id=1, source_target_pairs={{64,0},{128,64},{192,128},{65,1},{129,65},{193,129},{66,2},{130,66... | collective-permute-start | bytes 393224 | tf_op jit(solution)/shard_map/ppermute | solution.py:19
  13.9 18.1 %collective-permute-start.1 = (bf16[2,16,1,16,128]{4,3,2,1,0:T(8,128)(2,1)S(1)}, bf16[2,16,1,16,128]{4,3,2,1,0:T(8,128)(2,1)S(1)}, u32[]{:S(2)}, u32[]{:S(2)}) collective-permute-start(bf16[2,16,1,16,128]{4,3,2,1,0:T(8,128)(2,1)S(1)} %get-tuple-element.170), channel_id=1, source_target_pairs={{0,64},{64,128},{128,192},{1,65},{65,129},{129,193},{2,66},{66,130... | collective-permute-start | bytes 393224 | tf_op jit(solution)/shard_map/ppermute | solution.py:18
  34.9 15.0 %copy-start.23 = (s32[16,4]{0,1:T(4,128)S(1)}, s32[16,4]{0,1:T(4,128)}, u32[]{:S(2)}) copy-start(s32[16,4]{0,1:T(4,128)} %param.24) | copy-start | bytes 772
  36.8 22.5 %collective-permute-start.7 = (bf16[2,16,4,1,128]{4,3,2,1,0:T(2,128)(2,1)}, bf16[2,16,4,1,128]{4,3,2,1,0:T(2,128)(2,1)}, u32[]{:S(2)}, u32[]{:S(2)}) collective-permute-start(bf16[2,16,4,1,128]{4,3,2,1,0:T(2,128)(2,1)} %get-tuple-element.169), channel_id=1, source_target_pairs={{1,0},{2,1},{3,2},{4,3},{5,4},{6,5},{7,6},{8,7},{9,8},{10,9},{11,1... | collective-permute-start | bytes 98312 | tf_op jit(solution)/shard_map/ppermute | solution.py:19
  38.1 21.2 %collective-permute-start.4 = (bf16[2,16,4,1,128]{4,3,2,1,0:T(2,128)(2,1)}, bf16[2,16,4,1,128]{4,3,2,1,0:T(2,128)(2,1)}, u32[]{:S(2)}, u32[]{:S(2)}) collective-permute-start(bf16[2,16,4,1,128]{4,3,2,1,0:T(2,128)(2,1)} %get-tuple-element.168), channel_id=1, source_target_pairs={{0,1},{1,2},{2,3},{3,4},{4,5},{5,6},{6,7},{7,8},{8,9},{9,10},{10,1... | collective-permute-start | bytes 98312 | tf_op jit(solution)/shard_map/ppermute | solution.py:18
  42.7 16.6 %collective-permute-start.6 = (bf16[2,16,1,16,128]{4,3,2,1,0:T(8,128)(2,1)}, bf16[2,16,1,16,128]{4,3,2,1,0:T(8,128)(2,1)}, u32[]{:S(2)}, u32[]{:S(2)}) collective-permute-start(bf16[2,16,1,16,128]{4,3,2,1,0:T(8,128)(2,1)} %get-tuple-element.167), channel_id=1, source_target_pairs={{64,0},{128,64},{192,128},{65,1},{129,65},{193,129},{66,2},{130,66... | collective-permute-start | bytes 393224 | tf_op jit(solution)/shard_map/ppermute | solution.py:19
  44.6 14.7 %collective-permute-start.5 = (bf16[2,16,1,16,128]{4,3,2,1,0:T(8,128)(2,1)}, bf16[2,16,1,16,128]{4,3,2,1,0:T(8,128)(2,1)}, u32[]{:S(2)}, u32[]{:S(2)}) collective-permute-start(bf16[2,16,1,16,128]{4,3,2,1,0:T(8,128)(2,1)} %get-tuple-element.166), channel_id=1, source_target_pairs={{0,64},{64,128},{128,192},{1,65},{65,129},{129,193},{2,66},{66,130... | collective-permute-start | bytes 393224 | tf_op jit(solution)/shard_map/ppermute | solution.py:18
  63.2 2.8 %copy-start.17 = (f32[32,2048]{1,0:T(8,128)S(1)}, f32[32,2048]{1,0:T(8,128)}, u32[]{:S(2)}) copy-start(f32[32,2048]{1,0:T(8,128)} %custom-call) | copy-start | bytes 786436
  63.2 2.8 %copy-start.24 = (s32[16,128]{1,0:T(8,128)S(1)}, s32[16,128]{1,0:T(8,128)}, u32[]{:S(2)}) copy-start(s32[16,128]{1,0:T(8,128)} %param.23) | copy-start | bytes 24580
  79.1 3.1 %copy-start.16 = (bf16[2,16,16,128]{3,0,1,2:T(2,128)(2,1)}, bf16[2,16,16,128]{3,0,1,2:T(2,128)(2,1)S(1)}, u32[]{:S(2)}) copy-start(bf16[2,16,16,128]{3,0,1,2:T(2,128)(2,1)S(1)} %copy.142) | copy-start | bytes 393220
  82.9 27.2 %copy-start.2 = (f32[1024,2,32]{2,1,0:T(2,128)S(1)}, f32[1024,2,32]{2,1,0:T(2,128)}, u32[]{:S(2)}) copy-start(f32[1024,2,32]{2,1,0:T(2,128)} %gather_fusion) | copy-start | bytes 786436
  83.0 27.2 %copy-start.18 = (pred[128,8]{1,0:T(8,128)(4,1)S(1)}, pred[128,8]{1,0:T(8,128)(4,1)}, u32[]{:S(2)}) copy-start(pred[128,8]{1,0:T(8,128)(4,1)} %copy.106) | copy-start | bytes 3076
  94.0 26.8 %all-to-all-start = ((bf16[64,2,1024]{2,1,0:T(2,128)(2,1)}), bf16[64,2,1024]{2,1,0:T(2,128)(2,1)S(1)}, u32[]{:S(2)}, u32[]{:S(2)}) async-start(bf16[64,2,1024]{2,1,0:T(2,128)(2,1)} %reshape.176), calls=%async_computation | async-start | bytes 524288 | tf_op jit(solution)/shard_map/all_to_all | solution.py:197
  130.5 25.0 %all-to-all-start.1 = ((bf16[4,128,16,2,32]{1,4,3,2,0:T(8,128)(2,1)}), bf16[4,128,16,2,32]{1,4,3,2,0:T(8,128)(2,1)S(1)}, u32[]{:S(2)}, u32[]{:S(2)}) async-start(bf16[4,128,16,2,32]{1,4,3,2,0:T(8,128)(2,1)} %broadcast_in_dim.151), calls=%async_computation.1 | async-start | bytes 2097152 | tf_op jit(solution)/shard_map/all_to_all | solution.py:45
  135.0 16.3 %collective-permute-start.8 = (bf16[16,16,256]{2,1,0:T(8,128)(2,1)S(1)}, bf16[16,16,256]{2,1,0:T(8,128)(2,1)S(1)}, u32[]{:S(2)}, u32[]{:S(2)}) collective-permute-start(bf16[16,16,256]{2,1,0:T(8,128)(2,1)S(1)} %reshape.102), channel_id=1, source_target_pairs={{0,1},{1,2},{2,3},{3,4},{4,5},{5,6},{6,7},{7,8},{8,9},{9,10},{10,1... | collective-permute-start | bytes 393224 | tf_op jit(solution)/shard_map/ppermute | solution.py:37
  138.0 14.6 %collective-permute-start.9 = (bf16[16,16,256]{2,1,0:T(8,128)(2,1)S(1)}, bf16[16,16,256]{2,1,0:T(8,128)(2,1)S(1)}, u32[]{:S(2)}, u32[]{:S(2)}) collective-permute-start(bf16[16,16,256]{2,1,0:T(8,128)(2,1)S(1)} %reshape.102), channel_id=1, source_target_pairs={{1,0},{2,1},{3,2},{4,3},{5,4},{6,5},{7,6},{8,7},{9,8},{10,9},{11,1... | collective-permute-start | bytes 393224 | tf_op jit(solution)/shard_map/ppermute | solution.py:38
  173.9 5.9 %copy-start.6 = (f32[128,8,32]{2,1,0:T(8,128)S(1)}, f32[128,8,32]{2,1,0:T(8,128)}, u32[]{:S(2)}) copy-start(f32[128,8,32]{2,1,0:T(8,128)} %get-tuple-element.160) | copy-start | bytes 393220
  173.9 5.9 %copy-start.7 = (f32[128,8,32]{2,1,0:T(8,128)S(1)}, f32[128,8,32]{2,1,0:T(8,128)}, u32[]{:S(2)}) copy-start(f32[128,8,32]{2,1,0:T(8,128)} %get-tuple-element.161) | copy-start | bytes 393220
  187.2 18.4 %all-to-all-start.2 = ((bf16[64,2,1024]{2,1,0:T(2,128)(2,1)}), bf16[64,2,1024]{2,1,0:T(2,128)(2,1)S(1)}, u32[]{:S(2)}, u32[]{:S(2)}) async-start(bf16[64,2,1024]{2,1,0:T(2,128)(2,1)} %reshape.178), calls=%async_computation.2 | async-start | bytes 524288 | tf_op jit(solution)/shard_map/all_to_all | solution.py:209
  213.7 2.6 %copy-start.13 = (f32[8,2048]{1,0:T(8,128)S(1)}, f32[8,2048]{1,0:T(8,128)}, u32[]{:S(2)}) copy-start(f32[8,2048]{1,0:T(8,128)} %get-tuple-element.179) | copy-start | bytes 196612
  233.7 2.8 %copy-start.8 = (f32[16,16,256]{2,1,0:T(8,128)S(1)}, f32[16,16,256]{2,1,0:T(8,128)}, u32[]{:S(2)}) copy-start(f32[16,16,256]{2,1,0:T(8,128)} %fusion.46) | copy-start | bytes 786436
  233.7 2.8 %copy-start.9 = (f32[16,16,256]{2,1,0:T(8,128)S(1)}, f32[16,16,256]{2,1,0:T(8,128)}, u32[]{:S(2)}) copy-start(f32[16,16,256]{2,1,0:T(8,128)} %fusion.48) | copy-start | bytes 786436
  233.7 2.8 %copy-start.10 = (f32[16,16,256]{2,1,0:T(8,128)S(1)}, f32[16,16,256]{2,1,0:T(8,128)}, u32[]{:S(2)}) copy-start(f32[16,16,256]{2,1,0:T(8,128)} %fusion.50) | copy-start | bytes 786436
  233.7 2.8 %copy-start.15 = (bf16[16,16,256]{2,1,0:T(8,128)(2,1)S(1)}, bf16[16,16,256]{2,1,0:T(8,128)(2,1)}, u32[]{:S(2)}) copy-start(bf16[16,16,256]{2,1,0:T(8,128)(2,1)} %gather_fusion.2) | copy-start | bytes 393220
  (6 other events, 7.2 us)
where the time goes:
time: 240 us; the launch traced here: 238 us
  local copies, waits for them, and re-layouts  89.8 us (37%)
  starting transfers between devices  58.4 us (24%)
  other arithmetic  39.3 us (16%)
  matrix products  27.8 us (12%)
  waiting for transfers between devices  21.3 us (9%)
    ppermute x4, starting transfers between devices, extended(): lax.ppermute(last, axis, up)  17.6 us
    unnamed x58, local copies, waits for them, and re-layouts  16.5 us
    all_to_all x1, starting transfers between devices, shards(): lax.all_to_all(parent_patterns, 'shard', split_axis=3, concat_axis=0, til...  16.2 us
    dot_general x8, matrix products, add_block(): return total + jnp.dot(piece, selector, preferred_element_type=jnp.float32)  12.5 us
    gather x1, local copies, waits for them, and re-layouts, shards(): sources = jnp.take(gathered, target_ids, axis=0).astype(jnp.float32)  12 us
    ppermute x1, waiting for transfers between devices, padded_2(): before = lax.ppermute(last, axis, up)  12 us
    ppermute x4, starting transfers between devices, extended(): lax.ppermute(leading, axis, [(b, a) for a, b in up])  9.48 us
    all_to_all x1, waiting for transfers between devices, shards(): lax.all_to_all(parent_patterns, 'shard', split_axis=3, concat_axis=0, til...  9.3 us
  transfers between devices with their start and end apart: 13, of which 2 were waited for; matrix products, arithmetic and copies ran while one was open for 18% of the time, Pallas kernels for 0%

commit v1 on v0

--- a/solution.py
+++ b/solution.py
@@ -194,7 +194,16 @@
     cosine = jnp.cos(phase_angle)
     sine_part = jnp.sin(phase_angle)
     parent_patterns = aggregate(leaf, interp, cosine, sine_part)
-    directed = lax.all_to_all(parent_patterns, "shard", split_axis=3, concat_axis=0, tiled=True)
+    process_space = lambda in_array, which_axis, array_dim, k_dim: jnp.concatenate(
+        jax.lax.all_to_all(
+            jnp.stack(jnp.split(in_array, jax.lax.axis_size(which_axis), array_dim), axis=0),
+            split_axis=0,
+            axis_name=which_axis,
+            concat_axis=0,
+        ),
+        k_dim,
+    )
+    directed = process_space(parent_patterns, "shard", 3, 0)
     group_parents = directed.shape[0]
     group_index = lax.axis_index("space")
     target_ids = lax.dynamic_slice_in_dim(

time: 240 us -> 230 us (0.958)
  local copies, waits for them, and re-layouts: 89.8 us -> 75.9 us
  other arithmetic: 39.3 us -> 43.6 us
    all_to_all x2 -> x0, local copies, waits for them, and re-layouts: 6.08 us -> none  [shards(): lax.all_to_all(parent_patterns, 'shard', split_axis=3, concat_axis=0, til...]
    unnamed x58 -> x60, local copies, waits for them, and re-layouts: 16.5 us -> 11.3 us
    unnamed x2 -> x65, other arithmetic: 0.02 us -> 4.28 us
    another operation x1 -> x0, local copies, waits for them, and re-layouts: 3.68 us -> none  [aggregate(): return jnp.stack([real_part, imag_part], axis=2).astype(jnp.bfloat16)]
where the time goes in v1:
time: 230 us; the launch traced here: 229 us
  local copies, waits for them, and re-layouts  75.9 us (33%)
  starting transfers between devices  58.4 us (25%)
  other arithmetic  43.6 us (19%)
  matrix products  27.7 us (12%)
  waiting for transfers between devices  21.3 us (9%)
    ppermute x4, starting transfers between devices, extended(): lax.ppermute(last, axis, up)  17.6 us
    all_to_all x1, starting transfers between devices, shards(): jax.lax.all_to_all(jnp.stack(jnp.split(in_array, jax.lax.axis_size(which_...  16.2 us
    dot_general x8, matrix products, add_block(): return total + jnp.dot(piece, selector, preferred_element_type=jnp.float32)  12.5 us
    gather x1, local copies, waits for them, and re-layouts, shards(): sources = jnp.take(gathered, target_ids, axis=0).astype(jnp.float32)  12 us
    ppermute x1, waiting for transfers between devices, padded_2(): before = lax.ppermute(last, axis, up)  12 us
    unnamed x60, local copies, waits for them, and re-layouts  11.3 us
    ppermute x4, starting transfers between devices, extended(): lax.ppermute(leading, axis, [(b, a) for a, b in up])  9.48 us
    all_to_all x1, waiting for transfers between devices, shards(): jax.lax.all_to_all(jnp.stack(jnp.split(in_array, jax.lax.axis_size(which_...  9.29 us
  transfers between devices with their start and end apart: 13, of which 2 were waited for; matrix products, arithmetic and copies ran while one was open for 18% of the time, Pallas kernels for 0%

profile of v1, /device:TPU:1, one launch (start us, length us, event | category | flops | bytes accessed | tf_op | source)
XLA Modules:
  0.0 228.7 jit_solution(321347452824071284)
XLA Ops:
  4.2 4.6 %collective-permute-start = (bf16[2,16,4,1,128]{4,3,2,1,0:T(2,128)(2,1)S(1)}, bf16[2,16,4,1,128]{4,3,2,1,0:T(2,128)(2,1)S(1)}, u32[]{:S(2)}, u32[]{:S(2)}) collective-permute-start(bf16[2,16,4,1,128]{4,3,2,1,0:T(2,128)(2,1)S(1)} %get-tuple-element.172), channel_id=1, source_target_pairs={{0,1},{1,2},{2,3},{3,4},{4,5},{5,6},{6,7},{7,8},{8,9},{9,10},{10,1... | collective-permute-start | bytes 98312 | tf_op jit(solution)/shard_map/ppermute | solution.py:18
  8.9 5.0 %collective-permute-start.2 = (bf16[2,16,1,16,128]{4,3,2,1,0:T(8,128)(2,1)S(1)}, bf16[2,16,1,16,128]{4,3,2,1,0:T(8,128)(2,1)S(1)}, u32[]{:S(2)}, u32[]{:S(2)}) collective-permute-start(bf16[2,16,1,16,128]{4,3,2,1,0:T(8,128)(2,1)S(1)} %get-tuple-element.171), channel_id=1, source_target_pairs={{64,0},{128,64},{192,128},{65,1},{129,65},{193,129},{66,2},{130,66... | collective-permute-start | bytes 393224 | tf_op jit(solution)/shard_map/ppermute | solution.py:19
  13.9 3.0 %collective-permute-start.1 = (bf16[2,16,1,16,128]{4,3,2,1,0:T(8,128)(2,1)S(1)}, bf16[2,16,1,16,128]{4,3,2,1,0:T(8,128)(2,1)S(1)}, u32[]{:S(2)}, u32[]{:S(2)}) collective-permute-start(bf16[2,16,1,16,128]{4,3,2,1,0:T(8,128)(2,1)S(1)} %get-tuple-element.170), channel_id=1, source_target_pairs={{0,64},{64,128},{128,192},{1,65},{65,129},{129,193},{2,66},{66,130... | collective-permute-start | bytes 393224 | tf_op jit(solution)/shard_map/ppermute | solution.py:18
  21.7 5.1 %select_add_fusion.1 = (f32[4,16,128]{2,1,0:T(8,128)S(1)}, pred[4,16,128]{2,1,0:T(8,128)(4,1)S(1)}, pred[4,16,128]{2,1,0:T(8,128)(4,1)S(1)}, pred[4,16,128]{2,1,...) fusion(f32[]{:T(128)} %bitcast.7, f32[]{:T(128)} %bitcast.6, ...), kind=kLoop, calls=%fused_computation.310 | loop fusion | flops 196608 | bytes 131104 | tf_op jit(solution)/shard_map/add | solution.py:161
  26.7 5.0 %select_add_fusion = f32[4,16,128]{2,1,0:T(8,128)S(1)} fusion(pred[4,16,128]{2,1,0:T(8,128)(4,1)S(1)} %get-tuple-element.151, pred[4,16,128]{2,1,0:T(8,128)(4,1)S(1)} %get-tuple-element.150, pred[4,16,128]{2,1,0:T(8,128)(4,1)S(1)} %get-tuple-element.149, pred[4,16,128]{2,1,0:T(8,128)(4,1)S(1)} %get-tuple-element.148, ...), kind=kLoop, calls=%fused_computation.309 | loop fusion | flops 122880 | bytes 98336 | tf_op jit(solution)/shard_map/add | solution.py:162
  37.9 4.6 %collective-permute-start.4 = (bf16[2,16,4,1,128]{4,3,2,1,0:T(2,128)(2,1)}, bf16[2,16,4,1,128]{4,3,2,1,0:T(2,128)(2,1)}, u32[]{:S(2)}, u32[]{:S(2)}) collective-permute-start(bf16[2,16,4,1,128]{4,3,2,1,0:T(2,128)(2,1)} %get-tuple-element.168), channel_id=1, source_target_pairs={{0,1},{1,2},{2,3},{3,4},{4,5},{5,6},{6,7},{7,8},{8,9},{9,10},{10,1... | collective-permute-start | bytes 98312 | tf_op jit(solution)/shard_map/ppermute | solution.py:18
  42.5 1.9 collective-permute-start.6
  44.5 5.3 %collective-permute-start.5 = (bf16[2,16,1,16,128]{4,3,2,1,0:T(8,128)(2,1)}, bf16[2,16,1,16,128]{4,3,2,1,0:T(8,128)(2,1)}, u32[]{:S(2)}, u32[]{:S(2)}) collective-permute-start(bf16[2,16,1,16,128]{4,3,2,1,0:T(8,128)(2,1)} %get-tuple-element.166), channel_id=1, source_target_pairs={{0,64},{64,128},{128,192},{1,65},{65,129},{129,193},{2,66},{66,130... | collective-permute-start | bytes 393224 | tf_op jit(solution)/shard_map/ppermute | solution.py:18
  51.6 7.5 %gather_fusion = f32[1024,2,32]{2,1,0:T(2,128)} fusion(f32[316,2,32]{2,1,0:T(2,128)S(1)} %copy.82, s32[1024]{0:T(1024)S(1)} %broadcast_clamp_fusion.1), kind=kCustom, calls=%fused_computation.4 | custom fusion | bytes 528384 | tf_op jit(solution)/shard_map/jit(_take)/gather | solution.py:213
  65.9 12.9 %while.14 = (s32[]{:T(128)}, f32[32,2048]{1,0:T(8,128)S(1)}, bf16[32,8192]{1,0:T(8,128)(2,1)S(1)}, s32[16,128]{1,0:T(8,128)S(1)}, s32[]{:T(128)}, /*index=5*/s32[]{:T(128)}, s32[]{:T(128)}, s32[]{:T(128)}) while((s32[]{:T(128)}, f32[32,2048]{1,0:T(8,128)S(1)}, bf16[32,8192]{1,0:T(8,128)(2,1)S(1)}, s32[16,128]{1,0:T(8,128)S(1)}, ...), condition=%wide.region_1.2_spmd.clone, body=%wide.region_0.1_spmd.clone.sunk | while | flops 136446976 | bytes 606365 | solution.py:134
  88.2 3.1 %reshape.180 = bf16[64,2,1024]{2,1,0:T(2,128)(2,1)} reshape(bf16[64,2,2,16,32]{4,3,2,1,0:T(8,128)(2,1)} %bitcast.402) | data formatting | bytes 524288
  91.3 16.2 %all-to-all-start = ((bf16[64,2,1024]{2,1,0:T(2,128)(2,1)}), bf16[64,2,1024]{2,1,0:T(2,128)(2,1)S(1)}, u32[]{:S(2)}, u32[]{:S(2)}) async-start(bf16[64,2,1024]{2,1,0:T(2,128)(2,1)} %reshape.180), calls=%async_computation | async-start | bytes 524288 | tf_op jit(solution)/shard_map/all_to_all | solution.py:198
  108.7 9.3 %all-to-all-done = bf16[64,2,1024]{2,1,0:T(2,128)(2,1)S(1)} async-done(((bf16[64,2,1024]{2,1,0:T(2,128)(2,1)}), bf16[64,2,1024]{2,1,0:T(2,128)(2,1)S(1)}, u32[]{:S(2)}, u32[]{:S(2)}) %all-to-all-start) | async-done | bytes 262176 | tf_op jit(solution)/shard_map/all_to_all | solution.py:198
  120.9 3.5 %all-to-all-start.1 = ((bf16[4,128,16,2,32]{1,4,3,2,0:T(8,128)(2,1)}), bf16[4,128,16,2,32]{1,4,3,2,0:T(8,128)(2,1)S(1)}, u32[]{:S(2)}, u32[]{:S(2)}) async-start(bf16[4,128,16,2,32]{1,4,3,2,0:T(8,128)(2,1)} %broadcast_in_dim.151), calls=%async_computation.1 | async-start | bytes 2097152 | tf_op jit(solution)/shard_map/all_to_all | solution.py:45
  125.4 2.9 %collective-permute-start.8 = (bf16[16,16,256]{2,1,0:T(8,128)(2,1)S(1)}, bf16[16,16,256]{2,1,0:T(8,128)(2,1)S(1)}, u32[]{:S(2)}, u32[]{:S(2)}) collective-permute-start(bf16[16,16,256]{2,1,0:T(8,128)(2,1)S(1)} %reshape.105), channel_id=1, source_target_pairs={{0,1},{1,2},{2,3},{3,4},{4,5},{5,6},{6,7},{7,8},{8,9},{9,10},{10,1... | collective-permute-start | bytes 393224 | tf_op jit(solution)/shard_map/ppermute | solution.py:37
  129.7 12.0 %collective-permute-done.8 = bf16[16,16,256]{2,1,0:T(8,128)(2,1)S(1)} collective-permute-done((bf16[16,16,256]{2,1,0:T(8,128)(2,1)S(1)}, bf16[16,16,256]{2,1,0:T(8,128)(2,1)S(1)}, u32[]{:S(2)}, u32[]{:S(2)}) %collective-permute-start.8) | collective-permute-done | bytes 131104 | tf_op jit(solution)/shard_map/ppermute | solution.py:37
  143.7 2.2 gather_fusion.5
  145.9 6.4 %copy.88 = bf16[4,128,16,2,32]{4,2,3,1,0:T(8,128)(2,1)} copy(bf16[4,128,16,2,32]{1,4,3,2,0:T(8,128)(2,1)S(1)} %all-to-all-done.1) | data formatting | bytes 2097152 | tf_op jit(solution)/shard_map/all_to_all | solution.py:45
  152.3 12.0 %gather_fusion.1 = bf16[1024,16,2,32]{3,1,2,0:T(8,128)(2,1)} fusion(bf16[512,16,2,32]{3,1,2,0:T(8,128)(2,1)} %bitcast.396, s32[1024]{0:T(1024)S(1)} %broadcast_clamp_fusion), kind=kCustom, calls=%fused_computation.5 | custom fusion | bytes 4198400 | tf_op jit(solution)/shard_map/jit(_take)/gather | solution.py:215
  164.3 5.9 %fusion.11 = f32[128,8,16,2,32]{4,2,1,0,3:T(8,128)S(1)} fusion(bf16[128,8,16,2,32]{4,2,3,1,0:T(8,128)(2,1)} %bitcast.397, pred[128,8]{1,0:T(8,128)(4,1)S(1)} %copy.84), kind=kLoop, calls=%fused_computation.18 | loop fusion | flops 2097152 | bytes 6292480 | tf_op jit(solution)/shard_map/convert_element_type | solution.py:215
  170.2 3.8 %subtract_reduce_fusion = (bf16[128,16,32]{2,1,0:T(8,128)(2,1)S(1)}, bf16[128,16,32]{2,1,0:T(8,128)(2,1)S(1)}) fusion(f32[128,8,16,2,32]{4,2,1,0,3:T(8,128)S(1)} %fusion.11, f32[128,8,32]{2,1,0:T(8,128)S(1)} %copy-done.7, f32[128,8,32]{2,1,0:T(8,128)S(1)} %copy-done.6), kind=kLoop, calls=%fused_computation.20 | loop fusion | flops 4063232 | bytes 4718592 | tf_op jit(solution)/shard_map/reduce_sum | solution.py:99
  177.6 7.5 %all-to-all-start.2 = ((bf16[64,2,1024]{2,1,0:T(2,128)(2,1)}), bf16[64,2,1024]{2,1,0:T(2,128)(2,1)S(1)}, u32[]{:S(2)}, u32[]{:S(2)}) async-start(bf16[64,2,1024]{2,1,0:T(2,128)(2,1)} %reshape.182), calls=%async_computation.2 | async-start | bytes 524288 | tf_op jit(solution)/shard_map/all_to_all | solution.py:218
  185.1 1.9 fusion.46
  190.1 2.2 gather_fusion.2
  197.4 2.5 %copy.93 = f32[128,16,2,32]{3,1,2,0:T(8,128)} copy(bf16[128,16,2,32]{0,3,2,1:T(8,128)(2,1)S(1)} %copy.92) | data formatting | bytes 786432 | tf_op jit(solution)/shard_map/convert_element_type | solution.py:107
  199.9 4.2 %copy.94 = f32[2,16,2,64,32]{4,3,1,2,0:T(8,128)} copy(f32[2,16,2,64,32]{4,1,2,0,3:T(8,128)} %bitcast.398) | data formatting | bytes 1048576 | tf_op jit(solution)/shard_map/convert_element_type | solution.py:107
  204.1 2.5 %reshape.108 = f32[2,1,16,2,2048]{4,2,3,0,1:T(8,128)S(1)} reshape(f32[2,16,2,64,32]{4,3,1,2,0:T(8,128)} %copy.94) | data formatting | bytes 1048576 | tf_op jit(solution)/shard_map/convert_element_type | solution.py:107
  206.7 4.4 %add_convert_fusion = (bf16[2,8,16,1,2048]{4,3,2,1,0:T(2,128)(2,1)S(1)}, bf16[2,8,16,1,2048]{4,3,2,1,0:T(2,128)(2,1)S(1)}) fusion(f32[2,16,2048]{2,1,0:T(8,128)S(1)} %get-tuple-element.165, f32[8,2048]{1,0:T(8,128)S(1)} %copy-done.14, f32[2,16,2048]{2,1,0:T(8,128)S(1)} %get-tuple-element.164, f32[8,2048]{1,0:T(8,128)S(1)} %copy-done.12), kind=kLoop, calls=%fused_computation.159 | loop fusion | flops 4194304 | bytes 2752512 | tf_op jit(solution)/shard_map/convert.3
  211.1 5.2 %pad_maximum_fusion = bf16[2,8,16,2,2048]{4,3,2,1,0:T(2,128)(2,1)} fusion(bf16[2,8,16,1,2048]{4,3,2,1,0:T(2,128)(2,1)S(1)} %get-tuple-element.163, bf16[2,8,16,1,2048]{4,3,2,1,0:T(2,128)(2,1)S(1)} %get-tuple-element.162), kind=kLoop, calls=%fused_computation.155 | loop fusion | flops 4194304 | bytes 4194304 | tf_op jit(solution)/shard_map/stack | solution.py:112
  216.3 4.1 %convert_element_type.77 = bf16[512,2048]{1,0:T(8,128)(2,1)} reshape(bf16[2,8,16,2,2048]{4,3,2,1,0:T(2,128)(2,1)} %pad_maximum_fusion) | data formatting | bytes 4194304 | tf_op jit(solution)/shard_map/convert_element_type | solution.py:112
  220.4 3.7 %convolution_convert_fusion = bf16[512,512]{1,0:T(8,128)(2,1)} fusion(bf16[512,2048]{1,0:T(8,128)(2,1)} %convert_element_type.77, bf16[512,2048]{1,0:T(8,128)(2,1)S(1)} %copy-done), kind=kOutput, calls=%fused_computation.162 | convolution fusion | flops 1074003968 | bytes 4718592 | tf_op jit(solution)/shard_map/dot_general | solution.py:113
  226.8 1.9 fusion.26
  (210 shorter events, 67.5 us)
Async XLA Ops:
  0.6 80.2 %copy-start = (bf16[512,2048]{1,0:T(8,128)(2,1)S(1)}, bf16[512,2048]{1,0:T(8,128)(2,1)}, u32[]{:S(2)}) copy-start(bf16[512,2048]{1,0:T(8,128)(2,1)} %param.27) | copy-start | bytes 6291460
  0.6 16.3 %copy-start.15 = (bf16[2,128,512]{2,1,0:T(8,128)(2,1)S(1)}, bf16[2,128,512]{2,1,0:T(8,128)(2,1)}, u32[]{:S(2)}) copy-start(bf16[2,128,512]{2,1,0:T(8,128)(2,1)} %param.26) | copy-start | bytes 786436
  0.7 17.7 %copy-start.21 = (f32[8]{0:T(128)S(1)}, f32[8]{0:T(128)}, u32[]{:S(2)}) copy-start(f32[8]{0:T(128)} %param.21) | copy-start | bytes 100
  0.7 18.3 %copy-start.22 = (f32[8]{0:T(128)S(1)}, f32[8]{0:T(128)}, u32[]{:S(2)}) copy-start(f32[8]{0:T(128)} %param.22) | copy-start | bytes 100
  0.7 19.0 %copy-start.20 = (f32[8,2048]{1,0:T(8,128)S(1)}, f32[8,2048]{1,0:T(8,128)}, u32[]{:S(2)}) copy-start(f32[8,2048]{1,0:T(8,128)} %param.28) | copy-start | bytes 196612
  0.7 21.0 %copy-start.23 = (s32[4,16,128]{2,1,0:T(8,128)S(1)}, s32[4,16,128]{2,1,0:T(8,128)}, u32[]{:S(2)}) copy-start(s32[4,16,128]{2,1,0:T(8,128)} %param.20) | copy-start | bytes 98308
  2.9 28.9 %collective-permute-start.3 = (bf16[2,16,4,1,128]{4,3,2,1,0:T(2,128)(2,1)}, bf16[2,16,4,1,128]{4,3,2,1,0:T(2,128)(2,1)S(1)}, u32[]{:S(2)}, u32[]{:S(2)}) collective-permute-start(bf16[2,16,4,1,128]{4,3,2,1,0:T(2,128)(2,1)} %get-tuple-element.173), channel_id=1, source_target_pairs={{1,0},{2,1},{3,2},{4,3},{5,4},{6,5},{7,6},{8,7},{9,8},{10,9},{11,1... | collective-permute-start | bytes 98312 | tf_op jit(solution)/shard_map/ppermute | solution.py:19
  4.2 27.6 %collective-permute-start = (bf16[2,16,4,1,128]{4,3,2,1,0:T(2,128)(2,1)S(1)}, bf16[2,16,4,1,128]{4,3,2,1,0:T(2,128)(2,1)S(1)}, u32[]{:S(2)}, u32[]{:S(2)}) collective-permute-start(bf16[2,16,4,1,128]{4,3,2,1,0:T(2,128)(2,1)S(1)} %get-tuple-element.172), channel_id=1, source_target_pairs={{0,1},{1,2},{2,3},{3,4},{4,5},{5,6},{6,7},{7,8},{8,9},{9,10},{10,1... | collective-permute-start | bytes 98312 | tf_op jit(solution)/shard_map/ppermute | solution.py:18
  8.9 22.9 %collective-permute-start.2 = (bf16[2,16,1,16,128]{4,3,2,1,0:T(8,128)(2,1)S(1)}, bf16[2,16,1,16,128]{4,3,2,1,0:T(8,128)(2,1)S(1)}, u32[]{:S(2)}, u32[]{:S(2)}) collective-permute-start(bf16[2,16,1,16,128]{4,3,2,1,0:T(8,128)(2,1)S(1)} %get-tuple-element.171), channel_id=1, source_target_pairs={{64,0},{128,64},{192,128},{65,1},{129,65},{193,129},{66,2},{130,66... | collective-permute-start | bytes 393224 | tf_op jit(solution)/shard_map/ppermute | solution.py:19
  13.9 17.9 %collective-permute-start.1 = (bf16[2,16,1,16,128]{4,3,2,1,0:T(8,128)(2,1)S(1)}, bf16[2,16,1,16,128]{4,3,2,1,0:T(8,128)(2,1)S(1)}, u32[]{:S(2)}, u32[]{:S(2)}) collective-permute-start(bf16[2,16,1,16,128]{4,3,2,1,0:T(8,128)(2,1)S(1)} %get-tuple-element.170), channel_id=1, source_target_pairs={{0,64},{64,128},{128,192},{1,65},{65,129},{129,193},{2,66},{66,130... | collective-permute-start | bytes 393224 | tf_op jit(solution)/shard_map/ppermute | solution.py:18
  34.8 15.0 %copy-start.24 = (s32[16,4]{0,1:T(4,128)S(1)}, s32[16,4]{0,1:T(4,128)}, u32[]{:S(2)}) copy-start(s32[16,4]{0,1:T(4,128)} %param.24) | copy-start | bytes 772
  36.6 22.5 %collective-permute-start.7 = (bf16[2,16,4,1,128]{4,3,2,1,0:T(2,128)(2,1)}, bf16[2,16,4,1,128]{4,3,2,1,0:T(2,128)(2,1)}, u32[]{:S(2)}, u32[]{:S(2)}) collective-permute-start(bf16[2,16,4,1,128]{4,3,2,1,0:T(2,128)(2,1)} %get-tuple-element.169), channel_id=1, source_target_pairs={{1,0},{2,1},{3,2},{4,3},{5,4},{6,5},{7,6},{8,7},{9,8},{10,9},{11,1... | collective-permute-start | bytes 98312 | tf_op jit(solution)/shard_map/ppermute | solution.py:19
  37.9 21.2 %collective-permute-start.4 = (bf16[2,16,4,1,128]{4,3,2,1,0:T(2,128)(2,1)}, bf16[2,16,4,1,128]{4,3,2,1,0:T(2,128)(2,1)}, u32[]{:S(2)}, u32[]{:S(2)}) collective-permute-start(bf16[2,16,4,1,128]{4,3,2,1,0:T(2,128)(2,1)} %get-tuple-element.168), channel_id=1, source_target_pairs={{0,1},{1,2},{2,3},{3,4},{4,5},{5,6},{6,7},{7,8},{8,9},{9,10},{10,1... | collective-permute-start | bytes 98312 | tf_op jit(solution)/shard_map/ppermute | solution.py:18
  42.5 16.6 %collective-permute-start.6 = (bf16[2,16,1,16,128]{4,3,2,1,0:T(8,128)(2,1)}, bf16[2,16,1,16,128]{4,3,2,1,0:T(8,128)(2,1)}, u32[]{:S(2)}, u32[]{:S(2)}) collective-permute-start(bf16[2,16,1,16,128]{4,3,2,1,0:T(8,128)(2,1)} %get-tuple-element.167), channel_id=1, source_target_pairs={{64,0},{128,64},{192,128},{65,1},{129,65},{193,129},{66,2},{130,66... | collective-permute-start | bytes 393224 | tf_op jit(solution)/shard_map/ppermute | solution.py:19
  44.5 14.7 %collective-permute-start.5 = (bf16[2,16,1,16,128]{4,3,2,1,0:T(8,128)(2,1)}, bf16[2,16,1,16,128]{4,3,2,1,0:T(8,128)(2,1)}, u32[]{:S(2)}, u32[]{:S(2)}) collective-permute-start(bf16[2,16,1,16,128]{4,3,2,1,0:T(8,128)(2,1)} %get-tuple-element.166), channel_id=1, source_target_pairs={{0,64},{64,128},{128,192},{1,65},{65,129},{129,193},{2,66},{66,130... | collective-permute-start | bytes 393224 | tf_op jit(solution)/shard_map/ppermute | solution.py:18
  63.1 2.8 %copy-start.18 = (f32[32,2048]{1,0:T(8,128)S(1)}, f32[32,2048]{1,0:T(8,128)}, u32[]{:S(2)}) copy-start(f32[32,2048]{1,0:T(8,128)} %custom-call) | copy-start | bytes 786436
  63.1 2.8 %copy-start.25 = (s32[16,128]{1,0:T(8,128)S(1)}, s32[16,128]{1,0:T(8,128)}, u32[]{:S(2)}) copy-start(s32[16,128]{1,0:T(8,128)} %param.23) | copy-start | bytes 24580
  79.0 3.1 %copy-start.17 = (bf16[2,16,16,128]{3,0,1,2:T(2,128)(2,1)}, bf16[2,16,16,128]{3,0,1,2:T(2,128)(2,1)S(1)}, u32[]{:S(2)}) copy-start(bf16[2,16,16,128]{3,0,1,2:T(2,128)(2,1)S(1)} %copy.111) | copy-start | bytes 393220
  86.5 21.0 %copy-start.2 = (f32[1024,2,32]{2,1,0:T(2,128)S(1)}, f32[1024,2,32]{2,1,0:T(2,128)}, u32[]{:S(2)}) copy-start(f32[1024,2,32]{2,1,0:T(2,128)} %gather_fusion) | copy-start | bytes 786436
  86.5 21.0 %copy-start.19 = (pred[128,8]{1,0:T(8,128)(4,1)S(1)}, pred[128,8]{1,0:T(8,128)(4,1)}, u32[]{:S(2)}) copy-start(pred[128,8]{1,0:T(8,128)(4,1)} %copy.80) | copy-start | bytes 3076
  91.3 26.8 %all-to-all-start = ((bf16[64,2,1024]{2,1,0:T(2,128)(2,1)}), bf16[64,2,1024]{2,1,0:T(2,128)(2,1)S(1)}, u32[]{:S(2)}, u32[]{:S(2)}) async-start(bf16[64,2,1024]{2,1,0:T(2,128)(2,1)} %reshape.180), calls=%async_computation | async-start | bytes 524288 | tf_op jit(solution)/shard_map/all_to_all | solution.py:198
  120.9 25.0 %all-to-all-start.1 = ((bf16[4,128,16,2,32]{1,4,3,2,0:T(8,128)(2,1)}), bf16[4,128,16,2,32]{1,4,3,2,0:T(8,128)(2,1)S(1)}, u32[]{:S(2)}, u32[]{:S(2)}) async-start(bf16[4,128,16,2,32]{1,4,3,2,0:T(8,128)(2,1)} %broadcast_in_dim.151), calls=%async_computation.1 | async-start | bytes 2097152 | tf_op jit(solution)/shard_map/all_to_all | solution.py:45
  125.4 16.3 %collective-permute-start.8 = (bf16[16,16,256]{2,1,0:T(8,128)(2,1)S(1)}, bf16[16,16,256]{2,1,0:T(8,128)(2,1)S(1)}, u32[]{:S(2)}, u32[]{:S(2)}) collective-permute-start(bf16[16,16,256]{2,1,0:T(8,128)(2,1)S(1)} %reshape.105), channel_id=1, source_target_pairs={{0,1},{1,2},{2,3},{3,4},{4,5},{5,6},{6,7},{7,8},{8,9},{9,10},{10,1... | collective-permute-start | bytes 393224 | tf_op jit(solution)/shard_map/ppermute | solution.py:37
  128.4 14.6 %collective-permute-start.9 = (bf16[16,16,256]{2,1,0:T(8,128)(2,1)S(1)}, bf16[16,16,256]{2,1,0:T(8,128)(2,1)S(1)}, u32[]{:S(2)}, u32[]{:S(2)}) collective-permute-start(bf16[16,16,256]{2,1,0:T(8,128)(2,1)S(1)} %reshape.105), channel_id=1, source_target_pairs={{1,0},{2,1},{3,2},{4,3},{5,4},{6,5},{7,6},{8,7},{9,8},{10,9},{11,1... | collective-permute-start | bytes 393224 | tf_op jit(solution)/shard_map/ppermute | solution.py:38
  164.3 5.9 %copy-start.6 = (f32[128,8,32]{2,1,0:T(8,128)S(1)}, f32[128,8,32]{2,1,0:T(8,128)}, u32[]{:S(2)}) copy-start(f32[128,8,32]{2,1,0:T(8,128)} %get-tuple-element.160) | copy-start | bytes 393220
  164.3 5.9 %copy-start.7 = (f32[128,8,32]{2,1,0:T(8,128)S(1)}, f32[128,8,32]{2,1,0:T(8,128)}, u32[]{:S(2)}) copy-start(f32[128,8,32]{2,1,0:T(8,128)} %get-tuple-element.161) | copy-start | bytes 393220
  177.6 18.4 %all-to-all-start.2 = ((bf16[64,2,1024]{2,1,0:T(2,128)(2,1)}), bf16[64,2,1024]{2,1,0:T(2,128)(2,1)S(1)}, u32[]{:S(2)}, u32[]{:S(2)}) async-start(bf16[64,2,1024]{2,1,0:T(2,128)(2,1)} %reshape.182), calls=%async_computation.2 | async-start | bytes 524288 | tf_op jit(solution)/shard_map/all_to_all | solution.py:218
  204.1 2.6 %copy-start.14 = (f32[8,2048]{1,0:T(8,128)S(1)}, f32[8,2048]{1,0:T(8,128)}, u32[]{:S(2)}) copy-start(f32[8,2048]{1,0:T(8,128)} %get-tuple-element.179) | copy-start | bytes 196612
  224.0 2.8 %copy-start.9 = (f32[16,16,256]{2,1,0:T(8,128)S(1)}, f32[16,16,256]{2,1,0:T(8,128)}, u32[]{:S(2)}) copy-start(f32[16,16,256]{2,1,0:T(8,128)} %fusion.46) | copy-start | bytes 786436
  224.0 2.8 %copy-start.10 = (f32[16,16,256]{2,1,0:T(8,128)S(1)}, f32[16,16,256]{2,1,0:T(8,128)}, u32[]{:S(2)}) copy-start(f32[16,16,256]{2,1,0:T(8,128)} %fusion.48) | copy-start | bytes 786436
  224.0 2.8 %copy-start.11 = (f32[16,16,256]{2,1,0:T(8,128)S(1)}, f32[16,16,256]{2,1,0:T(8,128)}, u32[]{:S(2)}) copy-start(f32[16,16,256]{2,1,0:T(8,128)} %fusion.50) | copy-start | bytes 786436
  224.0 2.8 %copy-start.16 = (bf16[16,16,256]{2,1,0:T(8,128)(2,1)S(1)}, bf16[16,16,256]{2,1,0:T(8,128)(2,1)}, u32[]{:S(2)}) copy-start(bf16[16,16,256]{2,1,0:T(8,128)(2,1)} %gather_fusion.2) | copy-start | bytes 393220
  (7 other events, 8.1 us)
